TPU v7x, 16 devices: a 4x2x1 block of a 4x4x8 slice. The times are simulated.
16 devices in a mesh: rep: 2 (over y, z), pp: 8 (over x, core).
Axes of the slice: x: 4, y: 2, z: 1, core: 2. Of those that a mesh axis runs over, the one named last changes fastest.
The devices are a block of a 4x4x8 slice.
Arguments:
- x: bfloat16 [32, 512, 512], P('rep'), parts along dimension 0
- dy: bfloat16 [32, 512, 512], P('rep'), parts along dimension 0
- w_gate: bfloat16 [8, 512, 1536], P('pp')
- w_up: bfloat16 [8, 512, 1536], P('pp')
- w_down: bfloat16 [8, 1536, 512], P('pp')
Outputs:
- output 1: bfloat16 [16, 512, 1536], P(('rep', 'pp')), parts along dimension 0
- output 2: bfloat16 [16, 512, 1536], P(('rep', 'pp')), parts along dimension 0
- output 3: bfloat16 [16, 1536, 512], P(('rep', 'pp')), parts along dimension 0
There are 2 independent parts. A program takes and returns all parts, laid end to end along the dimension named above; an argument that names none is the same for every part.
All inputs are finite; a program needn't handle non-finite values.
Results may differ from a plain program's by a relative error of at most 0.0238.
Values are sent between devices in bfloat16 or wider.
A program may use at most 768 MiB of HBM per device.

v0:
```python
import jax
import jax.numpy as jnp
from jax import lax
from jax.sharding import PartitionSpec as P

NAMES = ("w_gate", "w_up", "w_down")


def matmul(a, w):
    return jnp.dot(a, w, preferred_element_type=jnp.float32).astype(jnp.bfloat16)


def normed(h):
    wide = h.astype(jnp.float32)
    scale = lax.rsqrt(jnp.mean(wide**2, -1, keepdims=True) + 1e-6)
    return (wide * scale).astype(jnp.bfloat16)


def layer(h, w):
    a = normed(h)
    gate = jnp.dot(a, w["w_gate"], preferred_element_type=jnp.float32)
    up = jnp.dot(a, w["w_up"], preferred_element_type=jnp.float32)
    return h + matmul((jax.nn.silu(gate) * up).astype(jnp.bfloat16), w["w_down"])


def stage(weights, h):
    for number in range(weights["w_gate"].shape[0]):
        h = layer(h, {name: w[number] for name, w in weights.items()})
    return h


def solution(mesh):
    stages = mesh.shape["pp"]
    onward = [(i, i + 1) for i in range(stages - 1)]
    back_again = [(i + 1, i) for i in range(stages - 1)]

    def step(x, dy, *arrays):
        weights = dict(zip(NAMES, arrays, strict=True))
        micro, me = x.shape[0], lax.axis_index("pp")
        kept, came = jnp.zeros_like(x), jnp.zeros_like(x[0])
        for t in range(micro + stages - 1):
            number = jnp.clip(t - me, 0, micro - 1)
            at_work = (t >= me) & (t - me < micro)
            h = jnp.where(me == 0, x[min(t, micro - 1)], came)
            was = lax.dynamic_index_in_dim(kept, number, 0, keepdims=False)
            kept = lax.dynamic_update_index_in_dim(kept, jnp.where(at_work, h, was), number, 0)
            came = lax.ppermute(stage(weights, h), "pp", onward)
        total = {name: jnp.zeros(w.shape, jnp.float32) for name, w in weights.items()}
        came, behind = jnp.zeros_like(x[0]), stages - 1 - me
        for t in range(micro + stages - 1):
            number = jnp.clip(t - behind, 0, micro - 1)
            at_work = (t >= behind) & (t - behind < micro)
            by_y = jnp.where(behind == 0, dy[min(t, micro - 1)], came)
            _, back = jax.vjp(stage, weights, lax.dynamic_index_in_dim(kept, number, 0, keepdims=False))
            by_w, by_h = back(by_y)
            total = {name: total[name] + jnp.where(at_work, by_w[name].astype(jnp.float32), 0.0) for name in NAMES}
            came = lax.ppermute(by_h, "pp", back_again)
        return tuple(total[name].astype(jnp.bfloat16) for name in NAMES)

    return jax.shard_map(
        step,
        mesh=mesh,
        in_specs=(P("rep", None, None),) * 2 + (P("pp", None, None),) * 3,
        out_specs=(P(("rep", "pp"), None, None),) * 3,
        check_vma=False,
    )
```

profile of v0, /device:TPU:113, one launch (start us, length us, event | category | flops | bytes accessed | tf_op | source)
XLA Modules:
  0.0 1144.4 jit_solution(10888905528127491401)
XLA Ops:
  6.0 5.3 fusion.834
  16.0 6.1 collective-permute-done
  26.8 5.7 fusion.831
  37.0 6.1 collective-permute-done.1
  47.9 5.7 fusion.828
  58.0 6.1 collective-permute-done.2
  68.9 5.7 fusion.825
  79.3 5.9 collective-permute-done.3
  90.0 5.8 fusion.822
  100.2 6.1 collective-permute-done.4
  111.0 5.7 fusion.819
  121.2 6.1 collective-permute-done.5
  132.1 5.7 fusion.816
  142.3 6.1 collective-permute-done.6
  153.1 5.7 fusion.813
  158.9 4.8 collective-permute-start.7
  163.7 5.7 collective-permute-done.7
  174.2 5.7 fusion.810
  184.4 6.1 collective-permute-done.8
  195.3 5.7 fusion.807
  205.5 6.0 collective-permute-done.9
  216.5 5.3 fusion.804
  240.5 5.3 fusion.801
  258.9 5.3 fusion.798
  280.6 5.3 fusion.795
  301.3 5.3 fusion.792
  322.0 5.3 fusion.789
  343.1 5.4 fusion.786
  363.4 5.4 fusion.783
  384.1 5.4 fusion.780
  404.8 5.4 fusion.777
  424.8 5.4 fusion.774
  445.3 5.4 fusion.771
  479.0 6.0 fusion.1007
  603.7 4.8 collective-permute-done.24
  678.6 4.8 collective-permute-done.27
  703.6 4.8 collective-permute-done.28
  778.5 4.8 collective-permute-done.31
  803.4 4.8 collective-permute-done.32
  878.2 4.8 collective-permute-done.35
  903.2 4.8 collective-permute-done.36
  978.0 4.8 collective-permute-done.39
  1003.0 4.8 collective-permute-done.40
  1053.0 4.8 collective-permute-done.42
  1079.0 5.0 collective-permute-done.43
  1090.3 17.4 %fusion.102 = bf16[1,512,1536]{2,1,0:T(8,128)(2,1)} fusion(bf16[512,1536]{1,0:T(8,128)(2,1)} %copy-done.105, bf16[512,1536]{1,0:T(8,128)(2,1)} %convolution_convert_fusion.46, bf16[512,1536]{1,0:T(8,128)(2,1)} %convolution_convert_fusion.47, bf16[512,1536]{1,0:T(8,128)(2,1)} %convolution_convert_fusion.48, ...), kind=kOutput, calls=%fused_computation.329 | convolution fusion | flops 865861632 | bytes 41420828 | tf_op jit(solution)/shard_map/transpose(jvp())/dot_general | solution.py:22
  1107.7 18.2 %fusion.101 = bf16[1,512,1536]{2,1,0:T(8,128)(2,1)} fusion(bf16[512,1536]{1,0:T(8,128)(2,1)} %fusion.74, bf16[512,1536]{1,0:T(8,128)(2,1)S(1)} %copy-done.108, bf16[512,1536]{1,0:T(8,128)(2,1)} %convolution_convert_fusion.69, bf16[512,1536]{1,0:T(8,128)(2,1)} %convolution_convert_fusion.70, bf16[512,1536]{1,0:T(8,128)(2,1)} %convolution_convert_fusion.71, ...), kind=kOutput, calls=%fused_computation.328 | convolution fusion | flops 860356608 | bytes 38275100 | tf_op jit(solution)/shard_map/transpose(jvp())/dot_general | solution.py:21
  1126.0 18.0 %fusion.100 = bf16[1,1536,512]{2,1,0:T(8,128)(2,1)} fusion(bf16[1536,512]{1,0:T(8,128)(2,1)} %convolution_convert_fusion.1, bf16[1536,512]{1,0:T(8,128)(2,1)} %convolution_convert_fusion.2, bf16[1536,512]{1,0:T(8,128)(2,1)} %convolution_convert_fusion.3, bf16[1536,512]{1,0:T(8,128)(2,1)} %convolution_convert_fusion.4, ...), kind=kOutput, calls=%fused_computation.327 | convolution fusion | flops 865337344 | bytes 43515928 | tf_op jit(solution)/shard_map/transpose(jvp())/dot_general | solution.py:10
  (668 shorter events, 841.7 us)
Async XLA Ops:
  11.4 10.7 collective-permute-start
  32.6 10.5 collective-permute-start.1
  53.6 10.5 collective-permute-start.2
  74.7 10.5 collective-permute-start.3
  95.7 10.5 collective-permute-start.4
  116.8 10.5 collective-permute-start.5
  137.8 10.5 collective-permute-start.6
  158.9 10.5 collective-permute-start.7
  180.0 10.5 collective-permute-start.8
  201.1 10.5 collective-permute-start.9
  221.9 13.8 %collective-permute-start.10 = (bf16[512,512]{1,0:T(8,128)(2,1)}, bf16[512,512]{1,0:T(8,128)(2,1)S(1)}, u32[]{:S(2)}, u32[]{:S(2)}) collective-permute-start(bf16[512,512]{1,0:T(8,128)(2,1)} %fusion.804), channel_id=1, source_target_pairs={{0,1},{1,2},{2,3},{3,4},{4,5},{5,6},{6,7},{8,9},{9,10},{10,11},{11... | collective-permute-start | bytes 1572872 | tf_op jit(solution)/shard_map/ppermute | solution.py:47
  245.8 8.0 collective-permute-start.11
  264.2 11.5 %collective-permute-start.12 = (bf16[512,512]{1,0:T(8,128)(2,1)}, bf16[512,512]{1,0:T(8,128)(2,1)S(1)}, u32[]{:S(2)}, u32[]{:S(2)}) collective-permute-start(bf16[512,512]{1,0:T(8,128)(2,1)} %fusion.798), channel_id=1, source_target_pairs={{0,1},{1,2},{2,3},{3,4},{4,5},{5,6},{6,7},{8,9},{9,10},{10,11},{11... | collective-permute-start | bytes 1572872 | tf_op jit(solution)/shard_map/ppermute | solution.py:47
  285.9 10.5 collective-permute-start.13
  306.6 10.5 collective-permute-start.14
  327.3 10.9 collective-permute-start.15
  348.4 10.1 collective-permute-start.16
  368.7 10.5 collective-permute-start.17
  389.5 10.5 collective-permute-start.18
  410.2 9.7 collective-permute-start.19
  430.2 10.3 collective-permute-start.20
  450.7 10.5 collective-permute-start.21
  485.2 60.3 %copy-start.39 = (f32[512]{0:T(512)}, f32[512]{0:T(512)S(1)}, u32[]{:S(2)}) copy-start(f32[512]{0:T(512)S(1)} %fusion.1383) | copy-start | bytes 6148
  485.2 56.5 %copy-start.41 = (f32[512]{0:T(512)}, f32[512]{0:T(512)S(1)}, u32[]{:S(2)}) copy-start(f32[512]{0:T(512)S(1)} %fusion.1382) | copy-start | bytes 6148
  485.2 52.7 %copy-start.43 = (f32[512]{0:T(512)}, f32[512]{0:T(512)S(1)}, u32[]{:S(2)}) copy-start(f32[512]{0:T(512)S(1)} %fusion.1381) | copy-start | bytes 6148
  485.3 49.0 %copy-start.45 = (f32[512]{0:T(512)}, f32[512]{0:T(512)S(1)}, u32[]{:S(2)}) copy-start(f32[512]{0:T(512)S(1)} %fusion.1380) | copy-start | bytes 6148
  486.9 66.6 %collective-permute-start.22 = (bf16[512,512]{1,0:T(8,128)(2,1)S(1)}, bf16[512,512]{1,0:T(8,128)(2,1)S(1)}, u32[]{:S(2)}, u32[]{:S(2)}) collective-permute-start(bf16[512,512]{1,0:T(8,128)(2,1)S(1)} %fusion.1105), channel_id=1, source_target_pairs={{1,0},{2,1},{3,2},{4,3},{5,4},{6,5},{7,6},{9,8},{10,9},{11,10},{12... | collective-permute-start | bytes 1572872 | tf_op jit(solution)/shard_map/ppermute | solution.py:57
  569.5 14.0 %collective-permute-start.23 = (bf16[512,512]{1,0:T(8,128)(2,1)S(1)}, bf16[512,512]{1,0:T(8,128)(2,1)S(1)}, u32[]{:S(2)}, u32[]{:S(2)}) collective-permute-start(bf16[512,512]{1,0:T(8,128)(2,1)S(1)} %fusion.1104), channel_id=1, source_target_pairs={{1,0},{2,1},{3,2},{4,3},{5,4},{6,5},{7,6},{9,8},{10,9},{11,10},{12... | collective-permute-start | bytes 1572872 | tf_op jit(solution)/shard_map/ppermute | solution.py:57
  598.0 10.6 collective-permute-start.24
  623.0 10.5 collective-permute-start.25
  648.0 10.5 collective-permute-start.26
  672.9 10.5 collective-permute-start.27
  697.9 10.5 collective-permute-start.28
  722.9 10.5 collective-permute-start.29
  747.8 10.5 collective-permute-start.30
  772.8 10.5 collective-permute-start.31
  797.7 10.5 collective-permute-start.32
  822.6 10.5 collective-permute-start.33
  847.6 10.5 collective-permute-start.34
  872.5 10.5 collective-permute-start.35
  897.4 10.5 collective-permute-start.36
  922.3 10.5 collective-permute-start.37
  947.3 10.5 collective-permute-start.38
  972.3 10.5 collective-permute-start.39
  997.2 10.5 collective-permute-start.40
  1022.2 10.5 collective-permute-start.41
  1047.3 10.5 collective-permute-start.42
  1073.5 10.5 collective-permute-start.43
  (107 other events, 717.4 us)
where the time goes:
time: 1160 us; the launch traced here: 1140 us
  matrix products  685 us (59%)
  waiting for transfers between devices  156 us (13%)
  starting transfers between devices  138 us (12%)
  other arithmetic  107 us (9%)
  local copies, waits for them, and re-layouts  53.9 us (5%)
    dot_general x90, matrix products, layer(): gate = jnp.dot(a, w['w_gate'], preferred_element_type=jnp.float32)  241 us
    dot_general x68, matrix products, layer(): up = jnp.dot(a, w['w_up'], preferred_element_type=jnp.float32)  228 us
    dot_general x68, matrix products, matmul(): jnp.dot(a, w, preferred_element_type=jnp.float32).astype(jnp.bfloat16)  216 us
    ppermute x22, waiting for transfers between devices, step(): came = lax.ppermute(by_h, 'pp', back_again)  94.3 us
    ppermute x22, starting transfers between devices, step(): came = lax.ppermute(stage(weights, h), 'pp', onward)  89 us
    ppermute x22, waiting for transfers between devices, step(): came = lax.ppermute(stage(weights, h), 'pp', onward)  62 us
    ppermute x22, starting transfers between devices, step(): came = lax.ppermute(by_h, 'pp', back_again)  48.5 us
    dynamic_update_slice x23, other arithmetic, step(): lax.dynamic_update_index_in_dim(kept, jnp.where(at_work, h, was), number, 0)  44.1 us
  transfers between devices with their start and end apart: 44, of which 33 were waited for; matrix products, arithmetic and copies ran while one was open for 20% of the time, Pallas kernels for 0%

commit v1 on v0

v1 whole, which is shorter than its diff:
```python
import functools

import jax
import jax.numpy as jnp
from jax import lax
from jax.experimental import pallas as pl
from jax.experimental.pallas import tpu as pltpu
from jax.sharding import PartitionSpec as P

F32, BF16 = jnp.float32, jnp.bfloat16
ROWS = 256
COLS = 256
SLOTS = 2
EPS = 1e-6


def lead(stages, me):
    table = [2, 3, 5, 6, 8, 9, 12, 13]
    ahead = 0
    for stage in range(stages):
        ahead = jnp.where(me == stage, table[min(stages - 1 - stage, len(table) - 1)], ahead)
    return ahead


def dot(a, b):
    return jnp.dot(a, b, preferred_element_type=F32)


def kernel(stages, x, dy, wg_in, wu_in, wd_in, og, ou, od, hp, hq, ha,
           wg, wu, wd, wgt, wut, wdt, acc_g, acc_u, acc_d, hs, ds, norm, turned, turned_dy,
           st_p, st_q, st_a, in_p, in_q, w_a, w_g, w_u, onward, back,
           sem_w, sem_h, sem_d, sem_f, sem_b, sem_st, sem_in, sem_act, sem_out):
    micro, tokens, d = x.shape
    ff = wg_in.shape[-1]
    chunks, tiles = tokens // ROWS, ff // COLS
    me = lax.axis_index("pp")
    first, last = me == 0, me == stages - 1
    inner = jnp.logical_not(last)
    later = jnp.logical_not(first)
    ahead = lead(stages, me)

    weights = [pltpu.make_async_copy(src.at[0], dst, sem_w.at[i]) for i, (src, dst) in enumerate(((wg_in, wg), (wu_in, wu), (wd_in, wd)))]
    for copy in weights:
        copy.start()

    def rows(c):
        return pl.ds(c * ROWS, ROWS)

    def load_x(i, c):
        return pltpu.make_async_copy(x.at[i, rows(c)], hs.at[i, rows(c)], sem_h.at[i, c])

    def load_dy(i, c):
        return pltpu.make_async_copy(dy.at[i, rows(c)], ds.at[i, rows(c)], sem_d.at[i, c])

    def send_h(i, c):
        slot = lax.rem(i, 2)
        return pltpu.make_async_remote_copy(onward.at[slot, c], hs.at[i, rows(c)], sem_f.at[slot, c], sem_h.at[i, c],
                                            device_id={"pp": me + 1}, device_id_type=pl.DeviceIdType.MESH)

    def send_d(i, c):
        return pltpu.make_async_remote_copy(back.at[c], ds.at[i, rows(c)], sem_b.at[c], sem_d.at[i, c],
                                            device_id={"pp": me - 1}, device_id_type=pl.DeviceIdType.MESH)

    def spill(i, c):
        return [pltpu.make_async_copy(src.at[c], dst.at[i, rows(c)], sem_st.at[k, c])
                for k, (src, dst) in enumerate(((st_p, hp), (st_q, hq), (st_a, ha)))]

    def fetch(i, c):
        return [pltpu.make_async_copy(src.at[i, rows(c)], dst.at[c], sem_in.at[k, c])
                for k, (src, dst) in enumerate(((hp, in_p), (hq, in_q)))]

    def fetch_act(i):
        slot = lax.rem(i, SLOTS)
        return pltpu.make_async_copy(ha.at[i], w_a.at[slot], sem_act.at[slot])

    @pl.when(first)
    def _():
        def body(i, _):
            for c in range(chunks):
                load_x(i, c).start()
            return 0
        lax.fori_loop(0, micro, body, 0)

    @pl.when(last)
    def _():
        def body(i, _):
            for c in range(chunks):
                load_dy(i, c).start()
            return 0
        lax.fori_loop(0, micro, body, 0)

    barrier = pltpu.get_barrier_semaphore()

    @pl.when(later)
    def _():
        pl.semaphore_signal(barrier, inc=1, device_id={"pp": me - 1}, device_id_type=pl.DeviceIdType.MESH)

    @pl.when(inner)
    def _():
        pl.semaphore_signal(barrier, inc=1, device_id={"pp": me + 1}, device_id_type=pl.DeviceIdType.MESH)

    for copy in weights:
        copy.wait()

    @pl.when(first | last)
    def _():
        pl.semaphore_wait(barrier, 1)

    @pl.when(later & inner)
    def _():
        pl.semaphore_wait(barrier, 2)

    def prepare():
        for n in range(tiles):
            cols = pl.ds(n * COLS, COLS)
            wgt[cols, :] = wg[:, cols].T
            wut[cols, :] = wu[:, cols].T
            wdt[:, cols] = wd[cols, :].T
            acc_g[:, cols] = jnp.zeros((d, COLS), F32)
            acc_u[:, cols] = jnp.zeros((d, COLS), F32)
            acc_d[:, cols] = jnp.zeros((d, COLS), F32)

    @pl.when(later)
    def _():
        prepare()

    def scale_of(wide):
        return lax.rsqrt(jnp.mean(wide * wide, -1, keepdims=True) + EPS)

    def forward(i, c):
        @pl.when(first)
        def _():
            load_x(i, c).wait()

        @pl.when(later)
        def _():
            send_h(i, c).wait_recv()

        wide = hs[i, rows(c), :].astype(F32)
        norm[...] = (wide * scale_of(wide)).astype(BF16)
        for n in range(tiles):
            cols = pl.ds(n * COLS, COLS)
            gate = dot(norm[...], wg[:, cols])
            up = dot(norm[...], wu[:, cols])
            sig = 1.0 / (1.0 + jnp.exp(-gate))
            silu = gate * sig
            st_p[c, :, cols] = silu
            st_q[c, :, cols] = up * (sig + silu * (1.0 - sig))
            st_a[c, :, cols] = (silu * up).astype(BF16)
        for copy in spill(i, c):
            copy.start()

        @pl.when(inner)
        def _():
            @pl.when(i > 1)
            def _():
                send_h(i - 2, c).wait_send()

            out = dot(st_a[c], wd[...]).astype(BF16)
            onward[lax.rem(i, 2), c] = (hs[i, rows(c), :].astype(F32) + out.astype(F32)).astype(BF16)
            send_h(i, c).start()

    def backward(i, c):
        slot = lax.rem(i, SLOTS)

        @pl.when(last)
        def _():
            load_dy(i, c).wait()

        @pl.when(inner)
        def _():
            send_d(i, c).wait_recv()

        for copy in fetch(i, c):
            copy.wait()
        for n in range(tiles):
            cols = pl.ds(n * COLS, COLS)
            by_act = dot(ds[i, rows(c), :], wdt[:, cols]).astype(BF16).astype(F32)
            w_g[slot, rows(c), cols] = (by_act * in_q[c, :, cols]).astype(BF16)
            w_u[slot, rows(c), cols] = (by_act * in_p[c, :, cols]).astype(BF16)

        @pl.when(later)
        def _():
            @pl.when(i > 0)
            def _():
                send_d(i - 1, c).wait_send()

            by_gate = dot(w_g[slot, rows(c), :], wgt[...]).astype(BF16)
            by_up = dot(w_u[slot, rows(c), :], wut[...]).astype(BF16)
            by_a = (by_gate.astype(F32) + by_up.astype(F32)).astype(BF16).astype(F32)
            wide = hs[i, rows(c), :].astype(F32)
            scale = scale_of(wide)
            along = jnp.mean(by_a * wide, -1, keepdims=True) * (scale * scale * scale)
            by_h = (by_a * scale - wide * along).astype(BF16)
            back[c] = (ds[i, rows(c), :].astype(F32) + by_h.astype(F32)).astype(BF16)
            send_d(i, c).start()

    def weight(i):
        slot = lax.rem(i, SLOTS)
        for c in range(chunks):
            wide = hs[i, rows(c), :].astype(F32)
            turned[:, rows(c)] = (wide * scale_of(wide)).astype(BF16).T
            turned_dy[:, rows(c)] = ds[i, rows(c), :].T
        fetch_act(i).wait()
        for n in range(tiles):
            cols = pl.ds(n * COLS, COLS)
            for acc, left, right in ((acc_g, turned, w_g), (acc_u, turned, w_u), (acc_d, turned_dy, w_a)):
                acc[:, cols] += dot(left[...], right[slot, :, cols]).astype(BF16).astype(F32)

    def step(t, _):
        @pl.when((t > 0) & (t <= micro))
        def _():
            for c in range(chunks):
                for copy in spill(t - 1, c):
                    copy.wait()

        @pl.when(t < micro)
        def _():
            for c in range(chunks):
                forward(t, c)

        @pl.when(first & (t == 0))
        def _():
            prepare()

        b = t - ahead

        @pl.when((b >= 0) & (b < micro))
        def _():
            fetch_act(b).start()
            for c in range(chunks):
                backward(b, c)

        @pl.when((b >= -1) & (b < micro - 1))
        def _():
            for c in range(chunks):
                for copy in fetch(b + 1, c):
                    copy.start()

        w = b - (SLOTS - 1)

        @pl.when((w >= 0) & (w < micro))
        def _():
            weight(w)
        return 0

    lax.fori_loop(0, micro + ahead + SLOTS - 1, step, 0)

    @pl.when(later)
    def _():
        for c in range(chunks):
            send_d(micro - 1, c).wait_send()

    @pl.when(inner)
    def _():
        for c in range(chunks):
            send_h(micro - 2, c).wait_send()
            send_h(micro - 1, c).wait_send()

    for n in range(tiles):
        cols = pl.ds(n * COLS, COLS)
        w_g[0, :, cols] = acc_g[:, cols].astype(BF16)
        w_u[0, :, cols] = acc_u[:, cols].astype(BF16)
        wd[cols, :] = acc_d[:, cols].astype(BF16).T
    results = [pltpu.make_async_copy(src, dst.at[0], sem_out.at[i]) for i, (src, dst) in enumerate(((w_g.at[0], og), (w_u.at[0], ou), (wd, od)))]
    for copy in results:
        copy.start()
    for copy in results:
        copy.wait()


def solution(mesh):
    stages = mesh.shape["pp"]

    def step(x, dy, w_gate, w_up, w_down):
        micro, tokens, d = x.shape
        ff = w_gate.shape[-1]
        chunks = tokens // ROWS
        hbm = pl.BlockSpec(memory_space=pl.ANY)
        vmem, dma = pltpu.VMEM, pltpu.SemaphoreType.DMA
        outs = pl.pallas_call(
            functools.partial(kernel, stages),
            out_shape=[
                jax.ShapeDtypeStruct(w_gate.shape, BF16),
                jax.ShapeDtypeStruct(w_up.shape, BF16),
                jax.ShapeDtypeStruct(w_down.shape, BF16),
                jax.ShapeDtypeStruct((micro, tokens, ff), F32),
                jax.ShapeDtypeStruct((micro, tokens, ff), F32),
                jax.ShapeDtypeStruct((micro, tokens, ff), BF16),
            ],
            in_specs=[hbm] * 5,
            out_specs=[hbm] * 6,
            scratch_shapes=[
                vmem((d, ff), BF16), vmem((d, ff), BF16), vmem((ff, d), BF16),
                vmem((ff, d), BF16), vmem((ff, d), BF16), vmem((d, ff), BF16),
                vmem((d, ff), F32), vmem((d, ff), F32), vmem((d, ff), F32),
                vmem((micro, tokens, d), BF16), vmem((micro, tokens, d), BF16),
                vmem((ROWS, d), BF16), vmem((d, tokens), BF16), vmem((d, tokens), BF16),
                vmem((chunks, ROWS, ff), F32), vmem((chunks, ROWS, ff), F32), vmem((chunks, ROWS, ff), BF16),
                vmem((chunks, ROWS, ff), F32), vmem((chunks, ROWS, ff), F32),
                vmem((SLOTS, tokens, ff), BF16), vmem((SLOTS, tokens, ff), BF16), vmem((SLOTS, tokens, ff), BF16),
                vmem((2, chunks, ROWS, d), BF16), vmem((chunks, ROWS, d), BF16),
                dma((3,)), dma((micro, chunks)), dma((micro, chunks)), dma((2, chunks)), dma((chunks,)),
                dma((3, chunks)), dma((2, chunks)), dma((SLOTS,)), dma((3,)),
            ],
            compiler_params=pltpu.CompilerParams(collective_id=0, has_side_effects=True, vmem_limit_bytes=67000000),
        )(x, dy, w_gate, w_up, w_down)
        return tuple(outs[:3])

    return jax.shard_map(
        step,
        mesh=mesh,
        in_specs=(P("rep", None, None),) * 2 + (P("pp", None, None),) * 3,
        out_specs=(P(("rep", "pp"), None, None),) * 3,
        check_vma=False,
    )
```

time: 1160 us -> 242 us (0.21)
  the two profiles are of different devices: /device:TPU:113 before, /device:TPU:112 now
where the time goes in v1:
time: 242 us
  Pallas kernels  236 us (98%)
  local copies, waits for them, and re-layouts  5.89 us (2%)
    pallas_call x1, Pallas kernels, step(): pl.pallas_call(functools.partial(kernel, stages), out_shape=[jax.ShapeDty...  236 us
    unnamed x7, local copies, waits for them, and re-layouts  5.89 us

profile of v1, /device:TPU:112, one launch (start us, length us, event | category | flops | bytes accessed | tf_op | source)
XLA Modules:
  0.0 242.3 jit_solution(18189428360829855039)
XLA Ops:
  0.6 235.8 %shard_map.76 = (bf16[1,512,1536]{2,1,0:T(8,128)(2,1)}, bf16[1,512,1536]{2,1,0:T(8,128)(2,1)}, bf16[1,1536,512]{2,1,0:T(8,128)(2,1)}, f32[16,512,1536]{2,1,0:T(8...) custom-call(bf16[16,512,512]{2,1,0:T(8,128)(2,1)} %x.1, bf16[16,512,512]{2,1,0:T(8,128)(2,1)} %dy.1, ...), custom_call_target="tpu_custom_call" | custom-call | tf_op jit(solution)/shard_map/pallas_call | solution.py:281
  236.4 0.0 copy-start.1
  236.4 2.8 %copy.11 = bf16[1,512,1536]{2,1,0:T(8,128)(2,1)} copy(bf16[1,512,1536]{2,1,0:T(8,128)(2,1)} %get-tuple-element.12) | data formatting | bytes 3145728
  239.2 0.0 copy-done.1
  239.2 0.0 copy-start
  239.2 1.1 copy.12
  240.4 0.8 copy-done
  241.2 1.1 copy.13
Async XLA Ops:
  236.4 2.8 %copy-start.1 = (bf16[1,512,1536]{2,1,0:T(8,128)(2,1)S(1)}, bf16[1,512,1536]{2,1,0:T(8,128)(2,1)}, u32[]{:S(2)}) copy-start(bf16[1,512,1536]{2,1,0:T(8,128)(2,1)} %get-tuple-element.13) | copy-start | bytes 4718596
  239.2 2.0 copy-start

commit v2 on v1

--- a/solution.py
+++ b/solution.py
@@ -127,17 +127,19 @@
     def scale_of(wide):
         return lax.rsqrt(jnp.mean(wide * wide, -1, keepdims=True) + EPS)
 
-    def forward(i, c):
-        @pl.when(first)
-        def _():
-            load_x(i, c).wait()
-
-        @pl.when(later)
-        def _():
-            send_h(i, c).wait_recv()
-
+    def weight(i, n, acc, left, right):
+        slot, cols = lax.rem(i, SLOTS), pl.ds(n * COLS, COLS)
+        acc[:, cols] += dot(left[slot], right[slot, :, cols]).astype(BF16).astype(F32)
+
+    def parts(tile_numbers):
+        return [(n, *arrays) for n in tile_numbers for arrays in ((acc_g, turned, w_g), (acc_u, turned, w_u), (acc_d, turned_dy, w_a))]
+
+    def forward(i, c, onwards, w):
+        fill = [] if w is None else parts([c])
         wide = hs[i, rows(c), :].astype(F32)
         norm[...] = (wide * scale_of(wide)).astype(BF16)
+        for part in fill[:2]:
+            weight(w, *part)
         for n in range(tiles):
             cols = pl.ds(n * COLS, COLS)
             gate = dot(norm[...], wg[:, cols])
@@ -147,101 +149,132 @@
             st_p[c, :, cols] = silu
             st_q[c, :, cols] = up * (sig + silu * (1.0 - sig))
             st_a[c, :, cols] = (silu * up).astype(BF16)
-        for copy in spill(i, c):
-            copy.start()
-
-        @pl.when(inner)
-        def _():
-            @pl.when(i > 1)
-            def _():
-                send_h(i - 2, c).wait_send()
-
+        for part in fill[2:]:
+            weight(w, *part)
+        if onwards:
             out = dot(st_a[c], wd[...]).astype(BF16)
             onward[lax.rem(i, 2), c] = (hs[i, rows(c), :].astype(F32) + out.astype(F32)).astype(BF16)
             send_h(i, c).start()
-
-    def backward(i, c):
+        for copy in spill(i, c):
+            copy.start()
+
+    def backward(i, c, w):
         slot = lax.rem(i, SLOTS)
-
-        @pl.when(last)
-        def _():
-            load_dy(i, c).wait()
-
-        @pl.when(inner)
-        def _():
-            send_d(i, c).wait_recv()
-
-        for copy in fetch(i, c):
-            copy.wait()
+        each = (tiles - chunks) // chunks
+        fill = [] if w is None else parts(range(chunks + c * each, chunks + (c + 1) * each))
+        wide = hs[i, rows(c), :].astype(F32)
+        scale = scale_of(wide)
+        turned[slot, :, rows(c)] = (wide * scale).astype(BF16).T
+        turned_dy[slot, :, rows(c)] = ds[i, rows(c), :].T
         for n in range(tiles):
             cols = pl.ds(n * COLS, COLS)
             by_act = dot(ds[i, rows(c), :], wdt[:, cols]).astype(BF16).astype(F32)
             w_g[slot, rows(c), cols] = (by_act * in_q[c, :, cols]).astype(BF16)
             w_u[slot, rows(c), cols] = (by_act * in_p[c, :, cols]).astype(BF16)
-
-        @pl.when(later)
-        def _():
-            @pl.when(i > 0)
-            def _():
-                send_d(i - 1, c).wait_send()
-
-            by_gate = dot(w_g[slot, rows(c), :], wgt[...]).astype(BF16)
-            by_up = dot(w_u[slot, rows(c), :], wut[...]).astype(BF16)
-            by_a = (by_gate.astype(F32) + by_up.astype(F32)).astype(BF16).astype(F32)
-            wide = hs[i, rows(c), :].astype(F32)
-            scale = scale_of(wide)
-            along = jnp.mean(by_a * wide, -1, keepdims=True) * (scale * scale * scale)
-            by_h = (by_a * scale - wide * along).astype(BF16)
-            back[c] = (ds[i, rows(c), :].astype(F32) + by_h.astype(F32)).astype(BF16)
-            send_d(i, c).start()
-
-    def weight(i):
-        slot = lax.rem(i, SLOTS)
-        for c in range(chunks):
-            wide = hs[i, rows(c), :].astype(F32)
-            turned[:, rows(c)] = (wide * scale_of(wide)).astype(BF16).T
-            turned_dy[:, rows(c)] = ds[i, rows(c), :].T
-        fetch_act(i).wait()
-        for n in range(tiles):
-            cols = pl.ds(n * COLS, COLS)
-            for acc, left, right in ((acc_g, turned, w_g), (acc_u, turned, w_u), (acc_d, turned_dy, w_a)):
-                acc[:, cols] += dot(left[...], right[slot, :, cols]).astype(BF16).astype(F32)
+        for part in fill[:2]:
+            weight(w, *part)
+        by_gate = dot(w_g[slot, rows(c), :], wgt[...]).astype(BF16)
+        by_up = dot(w_u[slot, rows(c), :], wut[...]).astype(BF16)
+        by_a = (by_gate.astype(F32) + by_up.astype(F32)).astype(BF16).astype(F32)
+        along = jnp.mean(by_a * wide, -1, keepdims=True) * (scale * scale * scale)
+        by_h = (by_a * scale - wide * along).astype(BF16)
+        back[c] = (ds[i, rows(c), :].astype(F32) + by_h.astype(F32)).astype(BF16)
+        for part in fill[2:]:
+            weight(w, *part)
 
     def step(t, _):
+        b = t - ahead
+        w = b - (SLOTS - 1)
+        has_f, has_b, has_w = t < micro, (b >= 0) & (b < micro), (w >= 0) & (w < micro)
+
+        @pl.when(has_w)
+        def _():
+            fetch_act(w).wait()
+
         @pl.when((t > 0) & (t <= micro))
         def _():
             for c in range(chunks):
                 for copy in spill(t - 1, c):
                     copy.wait()
 
-        @pl.when(t < micro)
-        def _():
-            for c in range(chunks):
-                forward(t, c)
+        @pl.when(has_b)
+        def _():
+            fetch_act(b).start()
+
+        for c in range(chunks):
+            @pl.when(has_f)
+            def _():
+                @pl.when(first)
+                def _():
+                    load_x(t, c).wait()
+
+                @pl.when(later)
+                def _():
+                    send_h(t, c).wait_recv()
+
+                @pl.when(inner & (t > 1))
+                def _():
+                    send_h(t - 2, c).wait_send()
+
+            for onwards in (True, False):
+                at = inner if onwards else last
+
+                @pl.when(has_f & at & has_w)
+                def _():
+                    forward(t, c, onwards, w)
+
+                @pl.when(has_f & at & jnp.logical_not(has_w))
+                def _():
+                    forward(t, c, onwards, None)
 
         @pl.when(first & (t == 0))
         def _():
             prepare()
 
-        b = t - ahead
-
-        @pl.when((b >= 0) & (b < micro))
-        def _():
-            fetch_act(b).start()
-            for c in range(chunks):
-                backward(b, c)
-
-        @pl.when((b >= -1) & (b < micro - 1))
-        def _():
-            for c in range(chunks):
+        @pl.when(has_w & jnp.logical_not(has_f))
+        def _():
+            for part in parts(range(chunks)):
+                weight(w, *part)
+
+        for c in range(chunks):
+            @pl.when(has_b)
+            def _():
+                @pl.when(last)
+                def _():
+                    load_dy(b, c).wait()
+
+                @pl.when(inner)
+                def _():
+                    send_d(b, c).wait_recv()
+
+                @pl.when(later & (b > 0))
+                def _():
+                    send_d(b - 1, c).wait_send()
+
+                for copy in fetch(b, c):
+                    copy.wait()
+
+            @pl.when(has_b & has_w)
+            def _():
+                backward(b, c, w)
+
+            @pl.when(has_b & jnp.logical_not(has_w))
+            def _():
+                backward(b, c, None)
+
+            @pl.when(has_b & later)
+            def _():
+                send_d(b, c).start()
+
+            @pl.when((b >= -1) & (b < micro - 1))
+            def _():
                 for copy in fetch(b + 1, c):
                     copy.start()
 
-        w = b - (SLOTS - 1)
-
-        @pl.when((w >= 0) & (w < micro))
-        def _():
-            weight(w)
+        @pl.when(has_w & jnp.logical_not(has_b))
+        def _():
+            for part in parts(range(chunks, tiles)):
+                weight(w, *part)
         return 0
 
     lax.fori_loop(0, micro + ahead + SLOTS - 1, step, 0)
@@ -295,7 +328,7 @@
                 vmem((ff, d), BF16), vmem((ff, d), BF16), vmem((d, ff), BF16),
                 vmem((d, ff), F32), vmem((d, ff), F32), vmem((d, ff), F32),
                 vmem((micro, tokens, d), BF16), vmem((micro, tokens, d), BF16),
-                vmem((ROWS, d), BF16), vmem((d, tokens), BF16), vmem((d, tokens), BF16),
+                vmem((ROWS, d), BF16), vmem((SLOTS, d, tokens), BF16), vmem((SLOTS, d, tokens), BF16),
                 vmem((chunks, ROWS, ff), F32), vmem((chunks, ROWS, ff), F32), vmem((chunks, ROWS, ff), BF16),
                 vmem((chunks, ROWS, ff), F32), vmem((chunks, ROWS, ff), F32),
                 vmem((SLOTS, tokens, ff), BF16), vmem((SLOTS, tokens, ff), BF16), vmem((SLOTS, tokens, ff), BF16),

time: 242 us -> 225 us (0.930)
  Pallas kernels: 236 us -> 218 us
    pallas_call x1, Pallas kernels: 236 us -> 218 us  [step(): pl.pallas_call(functools.partial(kernel, stages), out_shape=[jax.ShapeDty...]
where the time goes in v2:
time: 225 us
  Pallas kernels  218 us (97%)
  local copies, waits for them, and re-layouts  5.89 us (3%)
    pallas_call x1, Pallas kernels, step(): pl.pallas_call(functools.partial(kernel, stages), out_shape=[jax.ShapeDty...  218 us
    unnamed x7, local copies, waits for them, and re-layouts  5.89 us

profile of v2, /device:TPU:112, one launch (start us, length us, event | category | flops | bytes accessed | tf_op | source)
XLA Modules:
  0.0 224.7 jit_solution(1173105939370156202)
XLA Ops:
  0.6 218.1 %shard_map.76 = (bf16[1,512,1536]{2,1,0:T(8,128)(2,1)}, bf16[1,512,1536]{2,1,0:T(8,128)(2,1)}, bf16[1,1536,512]{2,1,0:T(8,128)(2,1)}, f32[16,512,1536]{2,1,0:T(8...) custom-call(bf16[16,512,512]{2,1,0:T(8,128)(2,1)} %x.1, bf16[16,512,512]{2,1,0:T(8,128)(2,1)} %dy.1, ...), custom_call_target="tpu_custom_call" | custom-call | tf_op jit(solution)/shard_map/pallas_call | solution.py:314
  218.8 0.0 copy-start.1
  218.8 2.8 %copy.11 = bf16[1,512,1536]{2,1,0:T(8,128)(2,1)} copy(bf16[1,512,1536]{2,1,0:T(8,128)(2,1)} %get-tuple-element.12) | data formatting | bytes 3145728
  221.6 0.0 copy-done.1
  221.6 0.0 copy-start
  221.6 1.1 copy.12
  222.7 0.8 copy-done
  223.5 1.1 copy.13
Async XLA Ops:
  218.8 2.8 %copy-start.1 = (bf16[1,512,1536]{2,1,0:T(8,128)(2,1)S(1)}, bf16[1,512,1536]{2,1,0:T(8,128)(2,1)}, u32[]{:S(2)}) copy-start(bf16[1,512,1536]{2,1,0:T(8,128)(2,1)} %get-tuple-element.13) | copy-start | bytes 4718596
  221.6 2.0 copy-start

commit v3 on v2

--- a/solution.py
+++ b/solution.py
@@ -15,7 +15,7 @@
 
 
 def lead(stages, me):
-    table = [2, 3, 5, 6, 8, 9, 12, 13]
+    table = [1, 2, 4, 5, 7, 8, 14, 16]
     ahead = 0
     for stage in range(stages):
         ahead = jnp.where(me == stage, table[min(stages - 1 - stage, len(table) - 1)], ahead)
@@ -40,8 +40,6 @@
     ahead = lead(stages, me)
 
     weights = [pltpu.make_async_copy(src.at[0], dst, sem_w.at[i]) for i, (src, dst) in enumerate(((wg_in, wg), (wu_in, wu), (wd_in, wd)))]
-    for copy in weights:
-        copy.start()
 
     def rows(c):
         return pl.ds(c * ROWS, ROWS)
@@ -70,8 +68,16 @@
                 for k, (src, dst) in enumerate(((hp, in_p), (hq, in_q)))]
 
     def fetch_act(i):
-        slot = lax.rem(i, SLOTS)
+        slot = lax.rem(i, SLOTS + 1)
         return pltpu.make_async_copy(ha.at[i], w_a.at[slot], sem_act.at[slot])
+
+    @pl.when(first)
+    def _():
+        for c in range(chunks):
+            load_x(0, c).start()
+
+    for copy in weights:
+        copy.start()
 
     @pl.when(first)
     def _():
@@ -79,7 +85,7 @@
             for c in range(chunks):
                 load_x(i, c).start()
             return 0
-        lax.fori_loop(0, micro, body, 0)
+        lax.fori_loop(1, micro, body, 0)
 
     @pl.when(last)
     def _():
@@ -127,9 +133,13 @@
     def scale_of(wide):
         return lax.rsqrt(jnp.mean(wide * wide, -1, keepdims=True) + EPS)
 
+    def term(i, n, left, right):
+        slot = lax.rem(i, SLOTS)
+        held = lax.rem(i, SLOTS + 1) if right is w_a else slot
+        return dot(left[slot], right[held, :, pl.ds(n * COLS, COLS)]).astype(BF16).astype(F32)
+
     def weight(i, n, acc, left, right):
-        slot, cols = lax.rem(i, SLOTS), pl.ds(n * COLS, COLS)
-        acc[:, cols] += dot(left[slot], right[slot, :, cols]).astype(BF16).astype(F32)
+        acc[:, pl.ds(n * COLS, COLS)] += term(i, n, left, right)
 
     def parts(tile_numbers):
         return [(n, *arrays) for n in tile_numbers for arrays in ((acc_g, turned, w_g), (acc_u, turned, w_u), (acc_d, turned_dy, w_a))]
@@ -146,17 +156,24 @@
             up = dot(norm[...], wu[:, cols])
             sig = 1.0 / (1.0 + jnp.exp(-gate))
             silu = gate * sig
-            st_p[c, :, cols] = silu
-            st_q[c, :, cols] = up * (sig + silu * (1.0 - sig))
-            st_a[c, :, cols] = (silu * up).astype(BF16)
+            slope = up * (sig + silu * (1.0 - sig))
+            act = (silu * up).astype(BF16)
+            if onwards:
+                st_p[c, :, cols] = silu
+                st_q[c, :, cols] = slope
+                st_a[c, :, cols] = act
+            else:
+                in_p[c, :, cols] = silu
+                in_q[c, :, cols] = slope
+                w_a[lax.rem(i, SLOTS + 1), rows(c), cols] = act
         for part in fill[2:]:
             weight(w, *part)
         if onwards:
             out = dot(st_a[c], wd[...]).astype(BF16)
             onward[lax.rem(i, 2), c] = (hs[i, rows(c), :].astype(F32) + out.astype(F32)).astype(BF16)
             send_h(i, c).start()
-        for copy in spill(i, c):
-            copy.start()
+            for copy in spill(i, c):
+                copy.start()
 
     def backward(i, c, w):
         slot = lax.rem(i, SLOTS)
@@ -185,21 +202,63 @@
     def step(t, _):
         b = t - ahead
         w = b - (SLOTS - 1)
-        has_f, has_b, has_w = t < micro, (b >= 0) & (b < micro), (w >= 0) & (w < micro)
-
-        @pl.when(has_w)
+        has_f, has_b, has_w = t < micro, (b >= 0) & (b < micro), w >= 0
+        fetches = inner & (b >= -1) & (b < micro - 1)
+        early = (ahead > 2) | (t > micro)
+
+        @pl.when(has_w & inner)
         def _():
             fetch_act(w).wait()
 
-        @pl.when((t > 0) & (t <= micro))
+        @pl.when(has_b & inner)
+        def _():
+            fetch_act(b).start()
+
+        for c in range(chunks):
+            @pl.when(has_b)
+            def _():
+                @pl.when(last)
+                def _():
+                    load_dy(b, c).wait()
+
+                @pl.when(later & (b > 0))
+                def _():
+                    send_d(b - 1, c).wait_send()
+
+                @pl.when(inner)
+                def _():
+                    for copy in fetch(b, c):
+                        copy.wait()
+                    send_d(b, c).wait_recv()
+
+            @pl.when(has_b & has_w)
+            def _():
+                backward(b, c, w)
+
+            @pl.when(has_b & jnp.logical_not(has_w))
+            def _():
+                backward(b, c, None)
+
+            @pl.when(has_b & later)
+            def _():
+                send_d(b, c).start()
+
+            @pl.when(fetches & early)
+            def _():
+                for copy in fetch(b + 1, c):
+                    copy.start()
+
+        @pl.when(inner & (t > 0) & (t <= micro))
         def _():
             for c in range(chunks):
                 for copy in spill(t - 1, c):
                     copy.wait()
 
-        @pl.when(has_b)
-        def _():
-            fetch_act(b).start()
+        @pl.when(fetches & jnp.logical_not(early))
+        def _():
+            for c in range(chunks):
+                for copy in fetch(b + 1, c):
+                    copy.start()
 
         for c in range(chunks):
             @pl.when(has_f)
@@ -235,54 +294,37 @@
         def _():
             for part in parts(range(chunks)):
                 weight(w, *part)
-
+        return 0
+
+    lax.fori_loop(0, micro + ahead, step, 0)
+
+    end = micro - 1
+
+    @pl.when(inner)
+    def _():
+        fetch_act(end).wait()
+
+    free = (micro - 2) % SLOTS
+    results = []
+    for part in range(2):
+        some = range(part * tiles // 2, (part + 1) * tiles // 2)
+        for n in some:
+            cols = pl.ds(n * COLS, COLS)
+            w_g[free, :, cols] = (acc_g[:, cols] + term(end, n, turned, w_g)).astype(BF16)
+            w_u[free, :, cols] = (acc_u[:, cols] + term(end, n, turned, w_u)).astype(BF16)
+            wd[cols, :] = (acc_d[:, cols] + term(end, n, turned_dy, w_a)).astype(BF16).T
+        span = pl.ds(some[0] * COLS, len(some) * COLS)
+        copies = [pltpu.make_async_copy(w_g.at[free, :, span], og.at[0, :, span], sem_out.at[0, part]),
+                  pltpu.make_async_copy(w_u.at[free, :, span], ou.at[0, :, span], sem_out.at[1, part]),
+                  pltpu.make_async_copy(wd.at[span], od.at[0, span], sem_out.at[2, part])]
+        for copy in copies:
+            copy.start()
+        results += copies
+
+    @pl.when(later)
+    def _():
         for c in range(chunks):
-            @pl.when(has_b)
-            def _():
-                @pl.when(last)
-                def _():
-                    load_dy(b, c).wait()
-
-                @pl.when(inner)
-                def _():
-                    send_d(b, c).wait_recv()
-
-                @pl.when(later & (b > 0))
-                def _():
-                    send_d(b - 1, c).wait_send()
-
-                for copy in fetch(b, c):
-                    copy.wait()
-
-            @pl.when(has_b & has_w)
-            def _():
-                backward(b, c, w)
-
-            @pl.when(has_b & jnp.logical_not(has_w))
-            def _():
-                backward(b, c, None)
-
-            @pl.when(has_b & later)
-            def _():
-                send_d(b, c).start()
-
-            @pl.when((b >= -1) & (b < micro - 1))
-            def _():
-                for copy in fetch(b + 1, c):
-                    copy.start()
-
-        @pl.when(has_w & jnp.logical_not(has_b))
-        def _():
-            for part in parts(range(chunks, tiles)):
-                weight(w, *part)
-        return 0
-
-    lax.fori_loop(0, micro + ahead + SLOTS - 1, step, 0)
-
-    @pl.when(later)
-    def _():
-        for c in range(chunks):
-            send_d(micro - 1, c).wait_send()
+            send_d(end, c).wait_send()
 
     @pl.when(inner)
     def _():
@@ -290,15 +332,20 @@
             send_h(micro - 2, c).wait_send()
             send_h(micro - 1, c).wait_send()
 
-    for n in range(tiles):
-        cols = pl.ds(n * COLS, COLS)
-        w_g[0, :, cols] = acc_g[:, cols].astype(BF16)
-        w_u[0, :, cols] = acc_u[:, cols].astype(BF16)
-        wd[cols, :] = acc_d[:, cols].astype(BF16).T
-    results = [pltpu.make_async_copy(src, dst.at[0], sem_out.at[i]) for i, (src, dst) in enumerate(((w_g.at[0], og), (w_u.at[0], ou), (wd, od)))]
     for copy in results:
+        copy.wait()
+
+
+def hand_over(*refs):
+    sources, results, held, sem_in, sem_out = refs[:3], refs[3:6], refs[6:9], refs[9], refs[10]
+    reads = [pltpu.make_async_copy(a, b, sem_in.at[i]) for i, (a, b) in enumerate(zip(sources, held, strict=True))]
+    writes = [pltpu.make_async_copy(a, b, sem_out.at[i]) for i, (a, b) in enumerate(zip(held, results, strict=True))]
+    for copy in reads:
         copy.start()
-    for copy in results:
+    for read, write in zip(reads, writes, strict=True):
+        read.wait()
+        write.start()
+    for copy in writes:
         copy.wait()
 
 
@@ -331,14 +378,21 @@
                 vmem((ROWS, d), BF16), vmem((SLOTS, d, tokens), BF16), vmem((SLOTS, d, tokens), BF16),
                 vmem((chunks, ROWS, ff), F32), vmem((chunks, ROWS, ff), F32), vmem((chunks, ROWS, ff), BF16),
                 vmem((chunks, ROWS, ff), F32), vmem((chunks, ROWS, ff), F32),
-                vmem((SLOTS, tokens, ff), BF16), vmem((SLOTS, tokens, ff), BF16), vmem((SLOTS, tokens, ff), BF16),
+                vmem((SLOTS + 1, tokens, ff), BF16), vmem((SLOTS, tokens, ff), BF16), vmem((SLOTS, tokens, ff), BF16),
                 vmem((2, chunks, ROWS, d), BF16), vmem((chunks, ROWS, d), BF16),
                 dma((3,)), dma((micro, chunks)), dma((micro, chunks)), dma((2, chunks)), dma((chunks,)),
-                dma((3, chunks)), dma((2, chunks)), dma((SLOTS,)), dma((3,)),
+                dma((3, chunks)), dma((2, chunks)), dma((SLOTS + 1,)), dma((3, 2)),
             ],
             compiler_params=pltpu.CompilerParams(collective_id=0, has_side_effects=True, vmem_limit_bytes=67000000),
         )(x, dy, w_gate, w_up, w_down)
-        return tuple(outs[:3])
+        shapes = [jax.ShapeDtypeStruct(w.shape, BF16) for w in (w_gate, w_up, w_down)]
+        return tuple(pl.pallas_call(
+            hand_over,
+            out_shape=shapes,
+            in_specs=[hbm] * 3,
+            out_specs=[hbm] * 3,
+            scratch_shapes=[vmem(a.shape, a.dtype) for a in shapes] + [dma((3,)), dma((3,))],
+        )(*outs[:3]))
 
     return jax.shard_map(
         step,

time: 225 us -> 216 us (0.960)
  local copies, waits for them, and re-layouts: 5.89 us -> 0 us
  Pallas kernels: 218 us -> 215 us
    pallas_call x1, Pallas kernels: 218 us -> 212 us  [step(): pl.pallas_call(functools.partial(kernel, stages), out_shape=[jax.ShapeDty...]
    unnamed x7 -> x0, local copies, waits for them, and re-layouts: 5.89 us -> none
    pallas_call x0 -> x1, Pallas kernels: none -> 3.64 us  [step(): pl.pallas_call(hand_over, out_shape=shapes, in_specs=[hbm] * 3, out_specs...]
where the time goes in v3:
time: 216 us
  Pallas kernels  215 us (100%)
    pallas_call x1, Pallas kernels, step(): pl.pallas_call(functools.partial(kernel, stages), out_shape=[jax.ShapeDty...  212 us

profile of v3, /device:TPU:112, one launch (start us, length us, event | category | flops | bytes accessed | tf_op | source)
XLA Modules:
  0.0 216.2 jit_solution(17055112539304542427)
XLA Ops:
  0.6 211.8 %shard_map.76 = (bf16[1,512,1536]{2,1,0:T(8,128)(2,1)}, bf16[1,512,1536]{2,1,0:T(8,128)(2,1)}, bf16[1,1536,512]{2,1,0:T(8,128)(2,1)}, f32[16,512,1536]{2,1,0:T(8...) custom-call(bf16[16,512,512]{2,1,0:T(8,128)(2,1)} %x.1, bf16[16,512,512]{2,1,0:T(8,128)(2,1)} %dy.1, ...), custom_call_target="tpu_custom_call" | custom-call | tf_op jit(solution)/shard_map/pallas_call | solution.py:361
  212.4 3.6 %shard_map.77 = (bf16[1,512,1536]{2,1,0:T(8,128)(2,1)}, bf16[1,512,1536]{2,1,0:T(8,128)(2,1)}, bf16[1,1536,512]{2,1,0:T(8,128)(2,1)}) custom-call(bf16[1,512,1536]{2,1,0:T(8,128)(2,1)} %get-tuple-element.6.refs_0_, bf16[1,512,1536]{2,1,0:T(8,128)(2,1)} %get-tuple-element.7.refs_1_, bf16[1,1536,512]{2,1,0:T(8,128)(2,1)} %get-tuple-element.8.refs_2_), custom_call_target="tpu_custom_call" | custom-call | tf_op jit(solution)/shard_map/pallas_call | solution.py:389

commit v4 on v3

--- a/solution.py
+++ b/solution.py
@@ -10,26 +10,28 @@
 F32, BF16 = jnp.float32, jnp.bfloat16
 ROWS = 256
 COLS = 256
-SLOTS = 2
 EPS = 1e-6
 
 
-def lead(stages, me):
-    table = [1, 2, 4, 5, 7, 8, 14, 16]
-    ahead = 0
+LEAD = (1, 2, 5, 6, 9, 10, 15, 16)
+LAG = (8, 8, 6, 8, 3, 2, 2, 2)
+
+
+def at_stage(table, stages, me):
+    number = 0
     for stage in range(stages):
-        ahead = jnp.where(me == stage, table[min(stages - 1 - stage, len(table) - 1)], ahead)
-    return ahead
+        number = jnp.where(me == stage, table[min(stages - 1 - stage, len(table) - 1)], number)
+    return number
 
 
 def dot(a, b):
     return jnp.dot(a, b, preferred_element_type=F32)
 
 
-def kernel(stages, x, dy, wg_in, wu_in, wd_in, og, ou, od, hp, hq, ha,
+def kernel(stages, x, dy, wg_in, wu_in, wd_in, og, ou, od, hp, hq, ha, hg, hu,
            wg, wu, wd, wgt, wut, wdt, acc_g, acc_u, acc_d, hs, ds, norm, turned, turned_dy,
-           st_p, st_q, st_a, in_p, in_q, w_a, w_g, w_u, onward, back,
-           sem_w, sem_h, sem_d, sem_f, sem_b, sem_st, sem_in, sem_act, sem_out):
+           st_p, st_q, st_a, st_g, st_u, in_p, in_q, w_a, w_g, w_u, onward, back,
+           sem_w, sem_h, sem_d, sem_f, sem_b, sem_st, sem_by, sem_in, sem_wt, sem_out):
     micro, tokens, d = x.shape
     ff = wg_in.shape[-1]
     chunks, tiles = tokens // ROWS, ff // COLS
@@ -37,7 +39,7 @@
     first, last = me == 0, me == stages - 1
     inner = jnp.logical_not(last)
     later = jnp.logical_not(first)
-    ahead = lead(stages, me)
+    ahead, lag = at_stage(LEAD, stages, me), at_stage(LAG, stages, me)
 
     weights = [pltpu.make_async_copy(src.at[0], dst, sem_w.at[i]) for i, (src, dst) in enumerate(((wg_in, wg), (wu_in, wu), (wd_in, wd)))]
 
@@ -59,17 +61,26 @@
         return pltpu.make_async_remote_copy(back.at[c], ds.at[i, rows(c)], sem_b.at[c], sem_d.at[i, c],
                                             device_id={"pp": me - 1}, device_id_type=pl.DeviceIdType.MESH)
 
+    def spill_act(i, c):
+        return pltpu.make_async_copy(st_a.at[c], ha.at[i, rows(c)], sem_st.at[2, c])
+
     def spill(i, c):
-        return [pltpu.make_async_copy(src.at[c], dst.at[i, rows(c)], sem_st.at[k, c])
-                for k, (src, dst) in enumerate(((st_p, hp), (st_q, hq), (st_a, ha)))]
+        return [pltpu.make_async_copy(src.at[c], dst.at[i, rows(c)], sem_st.at[k, c]) for k, (src, dst) in enumerate(((st_p, hp), (st_q, hq)))]
+
+    def spill_by(i, c):
+        return [pltpu.make_async_copy(src.at[c], dst.at[i, rows(c)], sem_by.at[k, c]) for k, (src, dst) in enumerate(((st_g, hg), (st_u, hu)))]
 
     def fetch(i, c):
         return [pltpu.make_async_copy(src.at[i, rows(c)], dst.at[c], sem_in.at[k, c])
                 for k, (src, dst) in enumerate(((hp, in_p), (hq, in_q)))]
 
-    def fetch_act(i):
-        slot = lax.rem(i, SLOTS + 1)
-        return pltpu.make_async_copy(ha.at[i], w_a.at[slot], sem_act.at[slot])
+    each = (tiles - chunks) // chunks
+    groups = [range(chunks + c * each, chunks + (c + 1) * each) for c in range(chunks)] + [range(chunks)]
+
+    def fetch_tiles(i, group):
+        span = pl.ds(groups[group][0] * COLS, len(groups[group]) * COLS)
+        return [pltpu.make_async_copy(src.at[i, :, span], dst.at[:, span], sem_wt.at[k, group])
+                for k, (src, dst) in enumerate(((hg, w_g), (hu, w_u), (ha, w_a)))]
 
     @pl.when(first)
     def _():
@@ -134,12 +145,16 @@
         return lax.rsqrt(jnp.mean(wide * wide, -1, keepdims=True) + EPS)
 
     def term(i, n, left, right):
-        slot = lax.rem(i, SLOTS)
-        held = lax.rem(i, SLOTS + 1) if right is w_a else slot
-        return dot(left[slot], right[held, :, pl.ds(n * COLS, COLS)]).astype(BF16).astype(F32)
+        return dot(left[lax.rem(i, 2)], right[:, pl.ds(n * COLS, COLS)]).astype(BF16).astype(F32)
 
     def weight(i, n, acc, left, right):
         acc[:, pl.ds(n * COLS, COLS)] += term(i, n, left, right)
+
+    def turn(i, c):
+        i = jnp.clip(i, 0, micro - 1)
+        wide = hs[i, rows(c), :].astype(F32)
+        turned[lax.rem(i, 2), :, rows(c)] = (wide * scale_of(wide)).astype(BF16).T
+        turned_dy[lax.rem(i, 2), :, rows(c)] = ds[i, rows(c), :].T
 
     def parts(tile_numbers):
         return [(n, *arrays) for n in tile_numbers for arrays in ((acc_g, turned, w_g), (acc_u, turned, w_u), (acc_d, turned_dy, w_a))]
@@ -161,11 +176,10 @@
             if onwards:
                 st_p[c, :, cols] = silu
                 st_q[c, :, cols] = slope
-                st_a[c, :, cols] = act
             else:
                 in_p[c, :, cols] = silu
                 in_q[c, :, cols] = slope
-                w_a[lax.rem(i, SLOTS + 1), rows(c), cols] = act
+            st_a[c, :, cols] = act
         for part in fill[2:]:
             weight(w, *part)
         if onwards:
@@ -174,24 +188,22 @@
             send_h(i, c).start()
             for copy in spill(i, c):
                 copy.start()
-
-    def backward(i, c, w):
-        slot = lax.rem(i, SLOTS)
-        each = (tiles - chunks) // chunks
-        fill = [] if w is None else parts(range(chunks + c * each, chunks + (c + 1) * each))
+        spill_act(i, c).start()
+
+    def backward(i, c, w, upcoming):
+        fill = [] if w is None else parts(groups[c])
         wide = hs[i, rows(c), :].astype(F32)
         scale = scale_of(wide)
-        turned[slot, :, rows(c)] = (wide * scale).astype(BF16).T
-        turned_dy[slot, :, rows(c)] = ds[i, rows(c), :].T
+        turn(upcoming, c)
         for n in range(tiles):
             cols = pl.ds(n * COLS, COLS)
             by_act = dot(ds[i, rows(c), :], wdt[:, cols]).astype(BF16).astype(F32)
-            w_g[slot, rows(c), cols] = (by_act * in_q[c, :, cols]).astype(BF16)
-            w_u[slot, rows(c), cols] = (by_act * in_p[c, :, cols]).astype(BF16)
+            st_g[c, :, cols] = (by_act * in_q[c, :, cols]).astype(BF16)
+            st_u[c, :, cols] = (by_act * in_p[c, :, cols]).astype(BF16)
         for part in fill[:2]:
             weight(w, *part)
-        by_gate = dot(w_g[slot, rows(c), :], wgt[...]).astype(BF16)
-        by_up = dot(w_u[slot, rows(c), :], wut[...]).astype(BF16)
+        by_gate = dot(st_g[c], wgt[...]).astype(BF16)
+        by_up = dot(st_u[c], wut[...]).astype(BF16)
         by_a = (by_gate.astype(F32) + by_up.astype(F32)).astype(BF16).astype(F32)
         along = jnp.mean(by_a * wide, -1, keepdims=True) * (scale * scale * scale)
         by_h = (by_a * scale - wide * along).astype(BF16)
@@ -201,18 +213,32 @@
 
     def step(t, _):
         b = t - ahead
-        w = b - (SLOTS - 1)
+        w = b - lag
         has_f, has_b, has_w = t < micro, (b >= 0) & (b < micro), w >= 0
         fetches = inner & (b >= -1) & (b < micro - 1)
         early = (ahead > 2) | (t > micro)
-
-        @pl.when(has_w & inner)
-        def _():
-            fetch_act(w).wait()
-
-        @pl.when(has_b & inner)
-        def _():
-            fetch_act(b).start()
+        next_w = w >= -1
+
+        def refill(group):
+            @pl.when(next_w)
+            def _():
+                for copy in fetch_tiles(w + 1, group):
+                    copy.start()
+
+        def ready(some):
+            @pl.when(has_w)
+            def _():
+                for group in some:
+                    for copy in fetch_tiles(w, group):
+                        copy.wait()
+
+        ready(range(chunks))
+
+        @pl.when((b > 0) & (b <= micro))
+        def _():
+            for c in range(chunks):
+                for copy in spill_by(b - 1, c):
+                    copy.wait()
 
         for c in range(chunks):
             @pl.when(has_b)
@@ -233,21 +259,42 @@
 
             @pl.when(has_b & has_w)
             def _():
-                backward(b, c, w)
+                backward(b, c, w, w + 1)
 
             @pl.when(has_b & jnp.logical_not(has_w))
             def _():
-                backward(b, c, None)
+                backward(b, c, None, w + 1)
 
             @pl.when(has_b & later)
             def _():
                 send_d(b, c).start()
+
+            @pl.when(has_b)
+            def _():
+                for copy in spill_by(b, c):
+                    copy.start()
 
             @pl.when(fetches & early)
             def _():
                 for copy in fetch(b + 1, c):
                     copy.start()
 
+        @pl.when(has_w & jnp.logical_not(has_b))
+        def _():
+            for c in range(chunks):
+                turn(w + 1, c)
+            for part in parts(range(chunks, tiles)):
+                weight(w, *part)
+
+        for group in range(chunks):
+            refill(group)
+        ready([chunks])
+
+        @pl.when((t > 0) & (t <= micro))
+        def _():
+            for c in range(chunks):
+                spill_act(t - 1, c).wait()
+
         @pl.when(inner & (t > 0) & (t <= micro))
         def _():
             for c in range(chunks):
@@ -294,28 +341,28 @@
         def _():
             for part in parts(range(chunks)):
                 weight(w, *part)
+
+        refill(chunks)
         return 0
 
-    lax.fori_loop(0, micro + ahead, step, 0)
+    lax.fori_loop(0, micro + ahead + lag - 1, step, 0)
 
     end = micro - 1
 
-    @pl.when(inner)
-    def _():
-        fetch_act(end).wait()
-
-    free = (micro - 2) % SLOTS
+    for group in range(chunks + 1):
+        for copy in fetch_tiles(end, group):
+            copy.wait()
     results = []
     for part in range(2):
         some = range(part * tiles // 2, (part + 1) * tiles // 2)
         for n in some:
             cols = pl.ds(n * COLS, COLS)
-            w_g[free, :, cols] = (acc_g[:, cols] + term(end, n, turned, w_g)).astype(BF16)
-            w_u[free, :, cols] = (acc_u[:, cols] + term(end, n, turned, w_u)).astype(BF16)
+            wg[:, cols] = (acc_g[:, cols] + term(end, n, turned, w_g)).astype(BF16)
+            wu[:, cols] = (acc_u[:, cols] + term(end, n, turned, w_u)).astype(BF16)
             wd[cols, :] = (acc_d[:, cols] + term(end, n, turned_dy, w_a)).astype(BF16).T
         span = pl.ds(some[0] * COLS, len(some) * COLS)
-        copies = [pltpu.make_async_copy(w_g.at[free, :, span], og.at[0, :, span], sem_out.at[0, part]),
-                  pltpu.make_async_copy(w_u.at[free, :, span], ou.at[0, :, span], sem_out.at[1, part]),
+        copies = [pltpu.make_async_copy(wg.at[:, span], og.at[0, :, span], sem_out.at[0, part]),
+                  pltpu.make_async_copy(wu.at[:, span], ou.at[0, :, span], sem_out.at[1, part]),
                   pltpu.make_async_copy(wd.at[span], od.at[0, span], sem_out.at[2, part])]
         for copy in copies:
             copy.start()
@@ -367,21 +414,24 @@
                 jax.ShapeDtypeStruct((micro, tokens, ff), F32),
                 jax.ShapeDtypeStruct((micro, tokens, ff), F32),
                 jax.ShapeDtypeStruct((micro, tokens, ff), BF16),
+                jax.ShapeDtypeStruct((micro, tokens, ff), BF16),
+                jax.ShapeDtypeStruct((micro, tokens, ff), BF16),
             ],
             in_specs=[hbm] * 5,
-            out_specs=[hbm] * 6,
+            out_specs=[hbm] * 8,
             scratch_shapes=[
                 vmem((d, ff), BF16), vmem((d, ff), BF16), vmem((ff, d), BF16),
                 vmem((ff, d), BF16), vmem((ff, d), BF16), vmem((d, ff), BF16),
                 vmem((d, ff), F32), vmem((d, ff), F32), vmem((d, ff), F32),
                 vmem((micro, tokens, d), BF16), vmem((micro, tokens, d), BF16),
-                vmem((ROWS, d), BF16), vmem((SLOTS, d, tokens), BF16), vmem((SLOTS, d, tokens), BF16),
-                vmem((chunks, ROWS, ff), F32), vmem((chunks, ROWS, ff), F32), vmem((chunks, ROWS, ff), BF16),
+                vmem((ROWS, d), BF16), vmem((2, d, tokens), BF16), vmem((2, d, tokens), BF16),
                 vmem((chunks, ROWS, ff), F32), vmem((chunks, ROWS, ff), F32),
-                vmem((SLOTS + 1, tokens, ff), BF16), vmem((SLOTS, tokens, ff), BF16), vmem((SLOTS, tokens, ff), BF16),
+                vmem((chunks, ROWS, ff), BF16), vmem((chunks, ROWS, ff), BF16), vmem((chunks, ROWS, ff), BF16),
+                vmem((chunks, ROWS, ff), F32), vmem((chunks, ROWS, ff), F32),
+                vmem((tokens, ff), BF16), vmem((tokens, ff), BF16), vmem((tokens, ff), BF16),
                 vmem((2, chunks, ROWS, d), BF16), vmem((chunks, ROWS, d), BF16),
                 dma((3,)), dma((micro, chunks)), dma((micro, chunks)), dma((2, chunks)), dma((chunks,)),
-                dma((3, chunks)), dma((2, chunks)), dma((SLOTS + 1,)), dma((3, 2)),
+                dma((3, chunks)), dma((2, chunks)), dma((2, chunks)), dma((3, chunks + 1)), dma((3, 2)),
             ],
             compiler_params=pltpu.CompilerParams(collective_id=0, has_side_effects=True, vmem_limit_bytes=67000000),
         )(x, dy, w_gate, w_up, w_down)

time: 216 us -> 225 us (1.042)
  Pallas kernels: 215 us -> 224 us
    pallas_call x1, Pallas kernels: 212 us -> 220 us  [step(): pl.pallas_call(functools.partial(kernel, stages), out_shape=[jax.ShapeDty...]
where the time goes in v4:
time: 225 us; the launch traced here: 224 us
  Pallas kernels  224 us (100%)
    pallas_call x1, Pallas kernels, step(): pl.pallas_call(functools.partial(kernel, stages), out_shape=[jax.ShapeDty...  220 us

profile of v4, /device:TPU:112, one launch (start us, length us, event | category | flops | bytes accessed | tf_op | source)
XLA Modules:
  0.0 224.5 jit_solution(10468801602773065695)
XLA Ops:
  0.6 220.0 %shard_map.76 = (bf16[1,512,1536]{2,1,0:T(8,128)(2,1)}, bf16[1,512,1536]{2,1,0:T(8,128)(2,1)}, bf16[1,1536,512]{2,1,0:T(8,128)(2,1)}, f32[16,512,1536]{2,1,0:T(8...) custom-call(bf16[16,512,512]{2,1,0:T(8,128)(2,1)} %x.1, ...), custom_call_target="tpu_custom_call" | custom-call | tf_op jit(solution)/shard_map/pallas_call | solution.py:408
  220.7 3.6 %shard_map.77 = (bf16[1,512,1536]{2,1,0:T(8,128)(2,1)}, bf16[1,512,1536]{2,1,0:T(8,128)(2,1)}, bf16[1,1536,512]{2,1,0:T(8,128)(2,1)}) custom-call(bf16[1,512,1536]{2,1,0:T(8,128)(2,1)} %get-tuple-element.6.refs_0_, bf16[1,512,1536]{2,1,0:T(8,128)(2,1)} %get-tuple-element.7.refs_1_, bf16[1,1536,512]{2,1,0:T(8,128)(2,1)} %get-tuple-element.8.refs_2_), custom_call_target="tpu_custom_call" | custom-call | tf_op jit(solution)/shard_map/pallas_call | solution.py:439

commit v5 on v4

--- a/solution.py
+++ b/solution.py
@@ -14,7 +14,7 @@
 
 
 LEAD = (1, 2, 5, 6, 9, 10, 15, 16)
-LAG = (8, 8, 6, 8, 3, 2, 2, 2)
+LAG = (10, 10, 8, 8, 4, 3, 2, 2)
 
 
 def at_stage(table, stages, me):
@@ -216,7 +216,6 @@
         w = b - lag
         has_f, has_b, has_w = t < micro, (b >= 0) & (b < micro), w >= 0
         fetches = inner & (b >= -1) & (b < micro - 1)
-        early = (ahead > 2) | (t > micro)
         next_w = w >= -1
 
         def refill(group):
@@ -231,8 +230,6 @@
                 for group in some:
                     for copy in fetch_tiles(w, group):
                         copy.wait()
-
-        ready(range(chunks))
 
         @pl.when((b > 0) & (b <= micro))
         def _():
@@ -241,6 +238,8 @@
                     copy.wait()
 
         for c in range(chunks):
+            ready([c])
+
             @pl.when(has_b)
             def _():
                 @pl.when(last)
@@ -265,6 +264,12 @@
             def _():
                 backward(b, c, None, w + 1)
 
+            @pl.when(has_w & jnp.logical_not(has_b))
+            def _():
+                turn(w + 1, c)
+                for part in parts(groups[c]):
+                    weight(w, *part)
+
             @pl.when(has_b & later)
             def _():
                 send_d(b, c).start()
@@ -274,38 +279,23 @@
                 for copy in spill_by(b, c):
                     copy.start()
 
-            @pl.when(fetches & early)
+            @pl.when((t > 0) & (t <= micro))
+            def _():
+                spill_act(t - 1, c).wait()
+
+            @pl.when(inner & (t > 0) & (t <= micro))
+            def _():
+                for copy in spill(t - 1, c):
+                    copy.wait()
+
+            @pl.when(fetches)
             def _():
                 for copy in fetch(b + 1, c):
                     copy.start()
 
-        @pl.when(has_w & jnp.logical_not(has_b))
-        def _():
-            for c in range(chunks):
-                turn(w + 1, c)
-            for part in parts(range(chunks, tiles)):
-                weight(w, *part)
-
-        for group in range(chunks):
-            refill(group)
+            refill(c)
+
         ready([chunks])
-
-        @pl.when((t > 0) & (t <= micro))
-        def _():
-            for c in range(chunks):
-                spill_act(t - 1, c).wait()
-
-        @pl.when(inner & (t > 0) & (t <= micro))
-        def _():
-            for c in range(chunks):
-                for copy in spill(t - 1, c):
-                    copy.wait()
-
-        @pl.when(fetches & jnp.logical_not(early))
-        def _():
-            for c in range(chunks):
-                for copy in fetch(b + 1, c):
-                    copy.start()
 
         for c in range(chunks):
             @pl.when(has_f)

time: 225 us -> 201 us (0.89)
  Pallas kernels: 224 us -> 200 us
    pallas_call x1, Pallas kernels: 220 us -> 196 us  [step(): pl.pallas_call(functools.partial(kernel, stages), out_shape=[jax.ShapeDty...]
where the time goes in v5:
time: 201 us
  Pallas kernels  200 us (100%)
    pallas_call x1, Pallas kernels, step(): pl.pallas_call(functools.partial(kernel, stages), out_shape=[jax.ShapeDty...  196 us

profile of v5, /device:TPU:112, one launch (start us, length us, event | category | flops | bytes accessed | tf_op | source)
XLA Modules:
  0.0 200.5 jit_solution(5560899459428391872)
XLA Ops:
  0.6 196.1 %shard_map.76 = (bf16[1,512,1536]{2,1,0:T(8,128)(2,1)}, bf16[1,512,1536]{2,1,0:T(8,128)(2,1)}, bf16[1,1536,512]{2,1,0:T(8,128)(2,1)}, f32[16,512,1536]{2,1,0:T(8...) custom-call(bf16[16,512,512]{2,1,0:T(8,128)(2,1)} %x.1, ...), custom_call_target="tpu_custom_call" | custom-call | tf_op jit(solution)/shard_map/pallas_call | solution.py:398
  196.7 3.6 %shard_map.77 = (bf16[1,512,1536]{2,1,0:T(8,128)(2,1)}, bf16[1,512,1536]{2,1,0:T(8,128)(2,1)}, bf16[1,1536,512]{2,1,0:T(8,128)(2,1)}) custom-call(bf16[1,512,1536]{2,1,0:T(8,128)(2,1)} %get-tuple-element.6.refs_0_, bf16[1,512,1536]{2,1,0:T(8,128)(2,1)} %get-tuple-element.7.refs_1_, bf16[1,1536,512]{2,1,0:T(8,128)(2,1)} %get-tuple-element.8.refs_2_), custom_call_target="tpu_custom_call" | custom-call | tf_op jit(solution)/shard_map/pallas_call | solution.py:429

commit v6 on v5

--- a/solution.py
+++ b/solution.py
@@ -13,8 +13,8 @@
 EPS = 1e-6
 
 
-LEAD = (1, 2, 5, 6, 9, 10, 15, 16)
-LAG = (10, 10, 8, 8, 4, 3, 2, 2)
+LEAD = (1, 2, 5, 6, 9, 10, 14, 16)
+LAG = (15, 14, 11, 10, 7, 6, 2, 2)
 
 
 def at_stage(table, stages, me):
@@ -215,6 +215,7 @@
         b = t - ahead
         w = b - lag
         has_f, has_b, has_w = t < micro, (b >= 0) & (b < micro), w >= 0
+        final = b == micro - 1
         fetches = inner & (b >= -1) & (b < micro - 1)
         next_w = w >= -1
 
@@ -256,11 +257,11 @@
                         copy.wait()
                     send_d(b, c).wait_recv()
 
-            @pl.when(has_b & has_w)
+            @pl.when(has_b & has_w & jnp.logical_not(final))
             def _():
                 backward(b, c, w, w + 1)
 
-            @pl.when(has_b & jnp.logical_not(has_w))
+            @pl.when(has_b & (jnp.logical_not(has_w) | final))
             def _():
                 backward(b, c, None, w + 1)
 
@@ -293,7 +294,19 @@
                 for copy in fetch(b + 1, c):
                     copy.start()
 
-            refill(c)
+            @pl.when(jnp.logical_not(final))
+            def _():
+                refill(c)
+
+        @pl.when(has_w & final)
+        def _():
+            for part in parts(range(chunks, tiles)):
+                weight(w, *part)
+
+        @pl.when(final)
+        def _():
+            for c in range(chunks):
+                refill(c)
 
         ready([chunks])
 

time: 201 us -> 200 us (level)
  the two profiles are of different devices: /device:TPU:112 before, /device:TPU:126 now
where the time goes in v6:
time: 200 us; the launch traced here: 199 us
  Pallas kernels  199 us (100%)
    pallas_call x1, Pallas kernels, step(): pl.pallas_call(functools.partial(kernel, stages), out_shape=[jax.ShapeDty...  195 us

profile of v6, /device:TPU:126, one launch (start us, length us, event | category | flops | bytes accessed | tf_op | source)
XLA Modules:
  0.0 199.5 jit_solution(1179262803750381004)
XLA Ops:
  0.6 195.0 %shard_map.76 = (bf16[1,512,1536]{2,1,0:T(8,128)(2,1)}, bf16[1,512,1536]{2,1,0:T(8,128)(2,1)}, bf16[1,1536,512]{2,1,0:T(8,128)(2,1)}, f32[16,512,1536]{2,1,0:T(8...) custom-call(bf16[16,512,512]{2,1,0:T(8,128)(2,1)} %x.1, ...), custom_call_target="tpu_custom_call" | custom-call | tf_op jit(solution)/shard_map/pallas_call | solution.py:411
  195.7 3.6 %shard_map.77 = (bf16[1,512,1536]{2,1,0:T(8,128)(2,1)}, bf16[1,512,1536]{2,1,0:T(8,128)(2,1)}, bf16[1,1536,512]{2,1,0:T(8,128)(2,1)}) custom-call(bf16[1,512,1536]{2,1,0:T(8,128)(2,1)} %get-tuple-element.6.refs_0_, bf16[1,512,1536]{2,1,0:T(8,128)(2,1)} %get-tuple-element.7.refs_1_, bf16[1,1536,512]{2,1,0:T(8,128)(2,1)} %get-tuple-element.8.refs_2_), custom_call_target="tpu_custom_call" | custom-call | tf_op jit(solution)/shard_map/pallas_call | solution.py:442
